TPU v7x, 32 devices: a whole 2x2x4 slice. The times are simulated.
32 devices in a mesh: depth: 8 (over z, x), rows: 4 (over y, core).
Axes of the slice: x: 2, y: 2, z: 4, core: 2. Of those that a mesh axis runs over, the one named last changes fastest.
Arguments:
- density: float32 [128, 64, 1024], P('depth', 'rows'), may hold values from 0 to 1
- bin_of_level: int32 [16], replicated, may hold values from 0 to 7
- absorb_bins: float32 [8], replicated, may hold values from 0.00234375 to 0.0625
- emit_bins: float32 [8], replicated, may hold values from 0.2 to 3
- occupancy: int32 [8, 4, 8], P('depth', 'rows'), may hold values 0 or 1
- col_offsets: int32 [1024], replicated, may hold values from 2 to 6
- row_offsets: int32 [64], P('rows'), may hold values from 2 to 6
Outputs:
- front_transmittance: float32 [8, 64, 1024], P('depth', 'rows')
- final_image: float32 [2, 64, 1024], P(None, 'rows')
All inputs are finite; a program needn't handle non-finite values. No bound on the sum of `occupancy` on one device may be relied on, other than what follows from the above.
Results may differ from a plain program's by a relative error of at most 0.0002.
Values sent between devices are 32-bit elements; how exact they have to be, the bound alone decides.
A program may use at most 64 MiB of HBM per device.

v0:
```python
import functools
import math

import jax
import jax.numpy as jnp
from jax import lax
from jax.experimental import pallas as pl
from jax.experimental.pallas import tpu as pltpu
from jax.sharding import PartitionSpec as P

LANES = 128
SUB = 8
MESH = pl.DeviceIdType.MESH


def repeat(count, body):
    if count <= 16:
        for i in range(count):
            body(i)
    else:
        lax.fori_loop(0, count, lambda i, c: (body(i), c)[1], 0)


def kernel(
    n_depth,
    n_rows,
    dens_hbm,
    bins_ref,
    absorb_ref,
    emit_ref,
    occ_ref,
    col_ref,
    row_ref,
    results,
    dens,
    below,
    row_send,
    row_halo,
    corner_send,
    corner,
    parts,
    gathered,
    answers,
    load_sem,
    halo_send_sem,
    halo_recv_sem,
    part_send_sem,
    part_recv_sem,
    ans_send_sem,
    ans_recv_sem,
):
    slab, rows, cols = dens.shape
    owners = parts.shape[1]
    width = cols // owners
    tiles = cols // LANES
    row_tiles = rows // SUB
    levels = bins_ref.shape[0]
    d = lax.axis_index("depth")
    r = lax.axis_index("rows")

    def shifted(dd, dr):
        return (lax.rem(d + dd + n_depth, n_depth), lax.rem(r + dr + n_rows, n_rows))

    load = pltpu.make_async_copy(dens_hbm, dens, load_sem)
    load.start()

    barrier = pltpu.get_barrier_semaphore()
    for dd, dr in ((0, -1), (0, 1), (-1, -1), (1, 1)):
        pl.semaphore_signal(barrier, inc=1, device_id=shifted(dd, dr), device_id_type=MESH)

    def greet(i):
        pl.semaphore_signal(
            barrier, inc=1, device_id=(lax.rem(d + 1 + i, n_depth), r), device_id_type=MESH
        )

    repeat(n_depth - 1, greet)

    @pl.when(d == n_depth - 1)
    def _():
        below[...] = jnp.zeros_like(below)

    @pl.when(r == n_rows - 1)
    def _():
        row_halo[...] = jnp.zeros_like(row_halo)

    @pl.when(jnp.logical_or(d == n_depth - 1, r == n_rows - 1))
    def _():
        corner[...] = jnp.zeros_like(corner)

    lane = lax.broadcasted_iota(jnp.int32, (SUB, LANES), 1)
    sub = lax.broadcasted_iota(jnp.int32, (SUB, LANES), 0)
    to_log2 = -math.log2(math.e)
    absorb = [absorb_ref[bins_ref[k]] * to_log2 for k in range(levels)]
    emit = [emit_ref[bins_ref[k]] for k in range(levels)]

    def hinges(values):
        steps = [values[k + 1] - values[k] for k in range(levels - 1)]
        bend = steps[:1] + [steps[k] - steps[k - 1] for k in range(1, levels - 1)]
        shift = values[0]
        for k in range(1, levels - 1):
            shift = shift - bend[k] * float(k)
        return shift, bend

    a_shift, a_bend = hinges(absorb)
    e_shift, e_bend = hinges(emit)
    occ = [occ_ref[0, 0, (c * LANES) // (cols // occ_ref.shape[2])].astype(jnp.float32) for c in range(tiles)]

    def row_weights(t):
        frac = jnp.zeros((SUB, LANES), jnp.float32)
        for y in range(SUB):
            frac = jnp.where(sub == y, row_ref[t * SUB + y].astype(jnp.float32), frac)
        frac = frac / 8.0
        gain = 0.5 * float(levels - 1)
        return gain * (1.0 - frac), gain * frac

    def col_weights(c):
        frac = col_ref[0:1, c * LANES : (c + 1) * LANES].astype(jnp.float32) / 8.0
        frac = jnp.broadcast_to(frac, (SUB, LANES))
        keep = 1.0 - frac
        if c == tiles - 1:
            frac = jnp.where(lane == LANES - 1, 0.0, frac)
        return keep, frac

    def resampled(own, following, rw, cws):
        mixed = []
        for c in range(tiles):
            block = own(c)
            up = jnp.where(sub == SUB - 1, following(c), pltpu.roll(block, SUB - 1, 0))
            mixed.append(rw[0] * block + rw[1] * up)
        turned = [pltpu.roll(m, LANES - 1, 1) for m in mixed]
        out = []
        for c in range(tiles):
            right = jnp.where(lane == LANES - 1, turned[(c + 1) % tiles], turned[c])
            out.append(cws[c][0] * mixed[c] + cws[c][1] * right)
        return out

    def shade(prev, now, state):
        through, depth, light = state
        new_through, new_depth, new_light = [], [], []
        for c in range(tiles):
            scaled = prev[c] + now[c]
            absorbed = a_shift + a_bend[0] * scaled
            emitted = e_shift + e_bend[0] * scaled
            for k in range(1, levels - 1):
                hinge = jnp.maximum(scaled, float(k))
                absorbed = absorbed + a_bend[k] * hinge
                emitted = emitted + e_bend[k] * hinge
            absorbed = absorbed * occ[c]
            after = through[c] * jnp.exp2(absorbed)
            new_light.append(light[c] + (through[c] - after) * emitted)
            new_depth.append(depth[c] + absorbed)
            new_through.append(after)
        return new_through, new_depth, new_light

    cws = [col_weights(c) for c in range(tiles)]

    def tile_of(c):
        return slice(c * LANES, (c + 1) * LANES)

    def plane(z, t, rw):
        def own(c):
            return dens[z, t * SUB : (t + 1) * SUB, tile_of(c)]

        def following(c):
            if t + 1 < row_tiles:
                nxt = dens[z, (t + 1) * SUB : (t + 1) * SUB + 1, tile_of(c)]
            else:
                nxt = row_halo[z, 0:1, tile_of(c)]
            return jnp.broadcast_to(nxt, (SUB, LANES))

        return resampled(own, following, rw, cws)

    def last_plane(t, rw):
        def own(c):
            return below[t * SUB : (t + 1) * SUB, tile_of(c)]

        def following(c):
            if t + 1 < row_tiles:
                nxt = below[(t + 1) * SUB : (t + 1) * SUB + 1, tile_of(c)]
            else:
                nxt = corner[0:1, tile_of(c)]
            return jnp.broadcast_to(nxt, (SUB, LANES))

        return resampled(own, following, rw, cws)

    def march(t, first, last, carry):
        rw = row_weights(t)
        if carry is None:
            ones = [jnp.ones((SUB, LANES), jnp.float32)] * tiles
            zeros = [jnp.zeros((SUB, LANES), jnp.float32)] * tiles
            carry = (plane(0, t, rw), (ones, zeros, zeros))

        def step(z, carry):
            prev, state = carry
            now = plane(z, t, rw)
            return now, shade(prev, now, state)

        return lax.fori_loop(first, last, step, carry)

    def finish(t, carry):
        prev, state = carry
        _, depth, light = shade(prev, last_plane(t, row_weights(t)), state)
        for c in range(tiles):
            j, at = (c * LANES) // width, (c * LANES) % width
            parts[t, j, 0, :, at : at + LANES] = depth[c]
            parts[t, j, 1, :, at : at + LANES] = light[c]

    load.wait()
    for z in range(slab):
        row_send[z] = dens[z, 0:1, :]
    corner_send[...] = dens[0, 0:1, :]
    half = slab // 2
    states = [None] * row_tiles
    states[0] = march(0, 1, half, None)

    pl.semaphore_wait(barrier, n_depth - 1 + 4)

    def halo(k, src, dst, dd, dr):
        return pltpu.make_async_remote_copy(
            src_ref=src,
            dst_ref=dst,
            send_sem=halo_send_sem.at[k],
            recv_sem=halo_recv_sem.at[k],
            device_id=shifted(dd, dr),
            device_id_type=MESH,
        )

    depth_copy = halo(0, dens.at[0], below, -1, 0)
    rows_copy = halo(1, row_send, row_halo, 0, -1)
    corner_copy = halo(2, corner_send, corner, -1, -1)
    sends = (
        (depth_copy, d > 0, d < n_depth - 1),
        (rows_copy, r > 0, r < n_rows - 1),
        (
            corner_copy,
            jnp.logical_and(d > 0, r > 0),
            jnp.logical_and(d < n_depth - 1, r < n_rows - 1),
        ),
    )
    for copy, sending, _ in sends:
        pl.when(sending)(copy.start)

    def other(i):
        return lax.rem(d + 1 + i, n_depth)

    def when_owner(index, body):
        if owners == n_depth:
            body()
        else:
            pl.when(index < owners)(body)

    def part_copy(t, owner, source):
        return pltpu.make_async_remote_copy(
            src_ref=parts.at[t, owner],
            dst_ref=gathered.at[t, source],
            send_sem=part_send_sem.at[t, owner],
            recv_sem=part_recv_sem.at[t, source],
            device_id=(owner, r),
            device_id_type=MESH,
        )

    def answer_copy(t, target, owner):
        return pltpu.make_async_remote_copy(
            src_ref=answers.at[t, target],
            dst_ref=results.at[t, owner],
            send_sem=ans_send_sem.at[t, target],
            recv_sem=ans_recv_sem.at[t, owner],
            device_id=(target, r),
            device_id_type=MESH,
        )

    def send_parts(t):
        def send(i):
            when_owner(other(i), lambda: part_copy(t, other(i), d).start())

        repeat(n_depth - 1, send)

    def compose(t):
        gathered[t, pl.ds(d, 1)] = parts[t, pl.ds(d, 1)]

        def arrived(i):
            part_copy(t, d, other(i)).wait_recv()

        repeat(n_depth - 1, arrived)

        def add(i, carry):
            total, radiance = carry
            front = jnp.exp2(total)
            answers[t, i, 0] = front
            return total + gathered[t, i, 0], radiance + front * gathered[t, i, 1]

        zero = jnp.zeros((SUB, width), jnp.float32)
        carry = (zero, zero)
        if n_depth <= 16:
            for i in range(n_depth):
                carry = add(i, carry)
        else:
            carry = lax.fori_loop(0, n_depth, add, carry)
        total, radiance = carry
        remaining = jnp.exp2(total)

        def fill(i):
            answers[t, i, 1] = radiance
            answers[t, i, 2] = remaining

        repeat(n_depth, fill)

        def reply(i):
            answer_copy(t, other(i), d).start()

        repeat(n_depth - 1, reply)
        results[t, pl.ds(d, 1)] = answers[t, pl.ds(d, 1)]

    states[0] = march(0, half, slab, states[0])
    pl.when(sends[1][2])(rows_copy.wait_recv)
    for t in range(row_tiles):
        last = t == row_tiles - 1
        if not last:
            states[t + 1] = march(t + 1, 1, half, None)
        if t == 0:
            pl.when(sends[0][2])(depth_copy.wait_recv)
            pl.when(sends[2][2])(corner_copy.wait_recv)
        finish(t, states[t])
        send_parts(t)
        if not last:
            states[t + 1] = march(t + 1, half, slab, states[t + 1])

    for t in range(row_tiles):
        when_owner(d, functools.partial(compose, t))

    for t in range(row_tiles):

        def collect(i):
            when_owner(other(i), lambda: answer_copy(t, d, other(i)).wait_recv())

        repeat(n_depth - 1, collect)

    for copy, sending, _ in sends:
        pl.when(sending)(copy.wait_send)

    for t in range(row_tiles):

        def sent(i):
            when_owner(other(i), lambda: part_copy(t, other(i), d).wait_send())
            when_owner(d, lambda: answer_copy(t, other(i), d).wait_send())

        repeat(n_depth - 1, sent)


def lay_out(results, front_ref, image_ref):
    row_tiles, owners, _, _, width = results.shape
    for t in range(row_tiles):
        for j in range(owners):
            tall, where = slice(t * SUB, (t + 1) * SUB), slice(j * width, (j + 1) * width)
            front_ref[0, tall, where] = results[t, j, 0]
            image_ref[0, tall, where] = results[t, j, 1]
            image_ref[1, tall, where] = results[t, j, 2]


def on_device(n_depth, n_rows, density, bin_of_level, absorb_bins, emit_bins, occupancy, col_offsets, row_offsets):
    slab, rows, cols = density.shape
    owners = 1
    while owners * 2 <= n_depth and cols % (owners * 2 * LANES) == 0:
        owners *= 2
    width = cols // owners
    row_tiles = rows // SUB
    smem = pl.BlockSpec(memory_space=pltpu.SMEM)
    vmem = pl.BlockSpec(memory_space=pltpu.VMEM)
    f32 = jnp.float32
    results = pl.pallas_call(
        functools.partial(kernel, n_depth, n_rows),
        out_shape=pltpu.VMEM((row_tiles, owners, 3, SUB, width), f32),
        in_specs=[pl.BlockSpec(memory_space=pl.ANY), smem, smem, smem, smem, vmem, smem],
        out_specs=vmem,
        scratch_shapes=[
            pltpu.VMEM((slab, rows, cols), f32),
            pltpu.VMEM((rows, cols), f32),
            pltpu.VMEM((slab, 1, cols), f32),
            pltpu.VMEM((slab, 1, cols), f32),
            pltpu.VMEM((1, cols), f32),
            pltpu.VMEM((1, cols), f32),
            pltpu.VMEM((row_tiles, owners, 2, SUB, width), f32),
            pltpu.VMEM((row_tiles, n_depth, 2, SUB, width), f32),
            pltpu.VMEM((row_tiles, n_depth, 3, SUB, width), f32),
            pltpu.SemaphoreType.DMA,
            pltpu.SemaphoreType.DMA((3,)),
            pltpu.SemaphoreType.DMA((3,)),
            pltpu.SemaphoreType.DMA((row_tiles, owners)),
            pltpu.SemaphoreType.DMA((row_tiles, n_depth)),
            pltpu.SemaphoreType.DMA((row_tiles, n_depth)),
            pltpu.SemaphoreType.DMA((row_tiles, owners)),
        ],
        compiler_params=pltpu.CompilerParams(collective_id=0, has_side_effects=True),
    )(
        density,
        bin_of_level,
        absorb_bins,
        emit_bins,
        occupancy,
        col_offsets.reshape(1, cols),
        row_offsets,
    )
    laid = results.transpose(2, 0, 3, 1, 4).reshape(3, rows, cols)
    return laid[:1], laid[1:]


def solution(mesh):
    placed = (P("depth", "rows", None), P(), P(), P(), P("depth", "rows", None), P(), P("rows"))
    return jax.shard_map(
        functools.partial(on_device, mesh.shape["depth"], mesh.shape["rows"]),
        mesh=mesh,
        in_specs=placed,
        out_specs=(P("depth", "rows", None), P(None, "rows", None)),
        check_vma=False,
    )
```

profile of v0, /device:TPU:0, one launch (start us, length us, event | category | flops | bytes accessed | tf_op | source)
XLA Modules:
  0.0 23.5 jit_solution(11414684008539108653)
XLA Ops:
  0.6 21.5 %shard_map.86 = f32[2,8,3,8,128]{4,3,2,1,0:T(8,128)S(1)} custom-call(f32[16,16,1024]{2,1,0:T(8,128)} %dens_hbm.1, s32[16]{0:T(128)} %bins_ref.1, f32[8]{0:T(128)} %absorb_ref.1, f32[8]{0:T(128)} %emit_ref.1, s32[1,1,8]{2,1,0:T(1,128)} %occ_ref.1, s32[1,1024]{1,0:T(1,128)} %bitcast.8, s32[16]{0:T(128)} %row_ref.1), custom_call_target="tpu_custom_call" | custom-call | tf_op jit(solution)/shard_map/pallas_call | solution.py:370
  22.1 0.6 %slice_bitcast_fusion = f32[1,16,1024]{2,1,0:T(8,128)} fusion(f32[3,2,8,8,128]{4,2,0,3,1:T(8,128)S(1)} %bitcast.6), kind=kLoop, calls=%fused_computation | loop fusion | bytes 131072 | tf_op jit(solution)/shard_map/slice | solution.py:404
  22.8 0.7 %slice.15 = f32[2,16,1024]{2,1,0:T(8,128)} reshape(f32[2,2,8,8,128]{4,3,2,1,0:T(8,128)S(1)} %copy.9) | data formatting | bytes 262144 | tf_op jit(solution)/shard_map/slice | solution.py:404
  (2 shorter events, 0.1 us)
where the time goes:
time: 23.7 us; the launch traced here: 23.5 us
  Pallas kernels  21.5 us (91%)
  local copies, waits for them, and re-layouts  1.37 us (6%)
  between operations  0.65 us (3%)
    pallas_call x1, Pallas kernels, on_device(): pl.pallas_call(functools.partial(kernel, n_depth, n_rows), out_shape=pltp...  21.5 us
    slice x4, local copies, waits for them, and re-layouts, on_device(): return (laid[:1], laid[1:])  1.37 us

commit v1 on v0

v1 whole, which is shorter than its diff:
```python
import functools
import math

import jax
import jax.numpy as jnp
from jax import lax
from jax.experimental import pallas as pl
from jax.experimental.pallas import tpu as pltpu
from jax.sharding import PartitionSpec as P

LANES = 128
SUB = 8
HALVES = 2
MESH = pl.DeviceIdType.MESH


def repeat(count, body):
    if count <= 16:
        for i in range(count):
            body(i)
    else:
        lax.fori_loop(0, count, lambda i, c: (body(i), c)[1], 0)


def pick(table, index):
    dims = lax.GatherDimensionNumbers(
        offset_dims=(),
        collapsed_slice_dims=(0,),
        start_index_map=(0,),
        operand_batching_dims=(1,),
        start_indices_batching_dims=(1,),
    )
    return lax.gather(
        table, index[..., None], dims, slice_sizes=(1, 1), mode=lax.GatherScatterMode.PROMISE_IN_BOUNDS
    )


def both(*conditions):
    return functools.reduce(jnp.logical_and, conditions)


def kernel(
    n_depth,
    n_rows,
    hosts,
    owners,
    dens_hbm,
    bins_hbm,
    absorb_hbm,
    emit_hbm,
    occ_hbm,
    col_hbm,
    row_hbm,
    front_ref,
    image_ref,
    dens,
    bins_ref,
    absorb_ref,
    emit_ref,
    occ_ref,
    col_ref,
    row_ref,
    row_send,
    row_halo,
    corner_send,
    corner,
    edge,
    state,
    parts,
    gathered,
    factors,
    pairs,
    factor_in,
    pair_in,
    load_sem,
    small_sem,
    depth_send_sem,
    depth_recv_sem,
    rows_send_sem,
    rows_recv_sem,
    corner_sem,
    part_send_sem,
    part_recv_sem,
    factor_send_sem,
    factor_recv_sem,
    pair_send_sem,
    pair_recv_sem,
):
    slab, rows, cols = dens_hbm.shape
    tiles = cols // LANES
    row_tiles = rows // SUB
    levels = bins_ref.shape[0]
    members = n_depth // HALVES
    per_owner = tiles // owners
    d = lax.axis_index("depth")
    r = lax.axis_index("rows")
    half = d // members
    m = lax.rem(d, members)
    slot = lax.rem(r, hosts)
    host_row = r - slot + hosts - 1
    is_host = slot == hosts - 1
    is_owner = both(is_host, m < owners)

    def load(c):
        return pltpu.make_async_copy(
            dens_hbm.at[:, :, c * LANES : (c + 1) * LANES],
            dens.at[c, pl.ds(0, slab), pl.ds(0, rows), :],
            load_sem.at[c],
        )

    small = [
        pltpu.make_async_copy(src, dst, small_sem.at[i])
        for i, (src, dst) in enumerate(
            (
                (bins_hbm, bins_ref),
                (absorb_hbm, absorb_ref),
                (emit_hbm, emit_ref),
                (occ_hbm, occ_ref),
                (col_hbm, col_ref),
                (row_hbm, row_ref),
            )
        )
    ]
    order = list(range(tiles - 1, -1, -1))
    for c in order:
        load(c).start()
    for copy in small:
        copy.start()

    barrier = pltpu.get_barrier_semaphore()

    def greet(dd, rr):
        pl.semaphore_signal(barrier, inc=1, device_id=(dd, rr), device_id_type=MESH)

    up_d, down_d = d > 0, d < n_depth - 1
    up_r, down_r = r > 0, r < n_rows - 1
    beside = (
        (up_d, d - 1, r),
        (up_r, d, r - 1),
        (both(up_d, up_r), d - 1, r - 1),
        (down_d, d + 1, r),
        (down_r, d, r + 1),
        (both(down_d, down_r), d + 1, r + 1),
    )
    expected = jnp.where(is_owner, n_depth * hosts - 1, HALVES * owners)
    for there, dd, rr in beside:
        pl.when(there)(functools.partial(greet, dd, rr))
        expected = expected + there.astype(jnp.int32)

    for s in range(hosts):

        def greet_block(j, s=s):
            wanted = is_owner
            if s == hosts - 1:
                wanted = jnp.logical_or(wanted, lax.rem(j, members) < owners)
            itself = both(j == d, slot == s)
            pl.when(both(wanted, jnp.logical_not(itself)))(
                functools.partial(greet, jnp.int32(j), host_row - hosts + 1 + s)
            )

        repeat(n_depth, greet_block)

    @pl.when(jnp.logical_not(down_d))
    def _():
        dens[:, slab] = jnp.zeros((tiles,) + dens.shape[2:], jnp.float32)

    lane = lax.broadcasted_iota(jnp.int32, (SUB, LANES), 1)
    sub = lax.broadcasted_iota(jnp.int32, (SUB, LANES), 0)
    last_lane = lane == LANES - 1

    for copy in small:
        copy.wait()

    def tables(values):
        values = values + values[-1:]
        out = []
        for first in range(0, levels, SUB):
            base = jnp.zeros((SUB, LANES), jnp.float32)
            slope = jnp.zeros((SUB, LANES), jnp.float32)
            for k in range(first, min(first + SUB, levels)):
                step = values[k + 1] - values[k]
                base = jnp.where(sub == k - first, values[k] - step * float(k), base)
                slope = jnp.where(sub == k - first, step, slope)
            out.append((base, slope))
        return out

    to_log2 = -math.log2(math.e)
    absorb = tables([absorb_ref[bins_ref[k]] * to_log2 for k in range(levels)])
    emit = tables([emit_ref[bins_ref[k]] for k in range(levels)])

    def absorb_of(c):
        occupied = occ_ref[0, 0, (c * LANES) // (cols // occ_ref.shape[2])].astype(jnp.float32)
        return [(base * occupied, slope * occupied) for base, slope in absorb]

    row_frac = []
    for t in range(row_tiles):
        frac = jnp.zeros((SUB, LANES), jnp.float32)
        for y in range(SUB):
            frac = jnp.where(sub == y, row_ref[t * SUB + y].astype(jnp.float32), frac)
        row_frac.append(frac / 8.0)

    def row_weights(t):
        if isinstance(t, int):
            frac = row_frac[t]
        else:
            frac = row_frac[-1]
            for i in range(row_tiles - 1):
                frac = jnp.where(t == i, row_frac[i], frac)
        gain = 0.5 * float(levels - 1)
        return gain * (1.0 - frac), gain * frac

    def col_weights(c):
        frac = jnp.broadcast_to(col_ref[c : c + 1, :].astype(jnp.float32) / 8.0, (SUB, LANES))
        keep = 1.0 - frac
        if c == tiles - 1:
            frac = jnp.where(last_lane, 0.0, frac)
        return keep, frac

    def rows_mixed(c, z, at, rw):
        return rw[0] * dens[c, z, pl.ds(at, SUB), :] + rw[1] * dens[c, z, pl.ds(at + 1, SUB), :]

    def cols_mixed(mixed, right_edge, cw):
        turned = pltpu.roll(mixed, LANES - 1, 1)
        return cw[0] * mixed + cw[1] * jnp.where(last_lane, right_edge, turned), turned

    def shade(prev, now, carry, absorb_c):
        through, depth, light = carry
        scaled = prev + now
        knot = lax.round(scaled - 0.5, lax.RoundingMethod.TO_NEAREST_EVEN).astype(jnp.int32)
        low = jnp.bitwise_and(knot, SUB - 1)

        def value(table):
            picked = [(pick(base, low), pick(slope, low)) for base, slope in table]
            base, slope = picked[-1]
            for i in range(len(picked) - 2, -1, -1):
                here = knot < (i + 1) * SUB
                base = jnp.where(here, picked[i][0], base)
                slope = jnp.where(here, picked[i][1], slope)
            return base + slope * scaled

        depth = depth + value(absorb_c)
        after = jnp.exp2(depth)
        light = light + (through - after) * value(emit)
        return after, depth, light

    zero = jnp.zeros((SUB, LANES), jnp.float32)
    one = jnp.ones((SUB, LANES), jnp.float32)

    def march(t):
        at = t * SUB
        if not isinstance(t, int):
            at = pl.multiple_of(at, SUB)
        rw = row_weights(t)
        for z in range(slab):
            edge[z] = zero
        for c in order:
            cw = col_weights(c)
            absorb_c = absorb_of(c)
            carry = (one, zero, zero)
            prev = None
            for z in range(slab):
                now, turned = cols_mixed(rows_mixed(c, z, at, rw), edge[z], cw)
                edge[z] = turned
                if prev is not None:
                    carry = shade(prev, now, carry, absorb_c)
                prev = now
            state[t, c, 0] = prev
            state[t, c, 1] = carry[1]
            state[t, c, 2] = carry[2]

    for c in order:
        load(c).wait()
        for z in range(slab):
            row_send[c, z : z + 1, :] = dens[c, z, 0:1, :]
        corner_send[c : c + 1, :] = dens[c, 0, 0:1, :]

    pl.semaphore_wait(barrier, expected)

    def remote(src, dst, send_sem, recv_sem, device):
        return pltpu.make_async_remote_copy(
            src_ref=src,
            dst_ref=dst,
            send_sem=send_sem,
            recv_sem=recv_sem,
            device_id=device,
            device_id_type=MESH,
        )

    def depth_copy(c):
        return remote(
            dens.at[c, 0, pl.ds(0, rows), :],
            dens.at[c, slab, pl.ds(0, rows), :],
            depth_send_sem.at[c],
            depth_recv_sem.at[c],
            (d - 1, r),
        )

    def rows_copy(c):
        return remote(row_send.at[c], row_halo.at[c], rows_send_sem.at[c], rows_recv_sem.at[c], (d, r - 1))

    corner_copy = remote(corner_send, corner, corner_sem.at[0], corner_sem.at[1], (d - 1, r - 1))

    @pl.when(up_d)
    def _():
        for c in order:
            depth_copy(c).start()

    @pl.when(up_r)
    def _():
        for c in order:
            rows_copy(c).start()

    pl.when(both(up_d, up_r))(corner_copy.start)

    for t in range(row_tiles):
        if t == row_tiles - 1:

            @pl.when(down_r)
            def _():
                for c in order:
                    rows_copy(c).wait_recv()
                    for z in range(slab):
                        dens[c, z, rows : rows + 1, :] = row_halo[c, z : z + 1, :]

            @pl.when(jnp.logical_not(down_r))
            def _():
                for c in order:
                    for z in range(slab):
                        dens[c, z, rows : rows + 1, :] = jnp.zeros((1, LANES), jnp.float32)

        march(t)

    @pl.when(both(down_d, down_r))
    def _():
        corner_copy.wait_recv()
        for c in order:
            dens[c, slab, rows : rows + 1, :] = corner[c : c + 1, :]

    @pl.when(both(down_d, jnp.logical_not(down_r)))
    def _():
        for c in order:
            dens[c, slab, rows : rows + 1, :] = jnp.zeros((1, LANES), jnp.float32)

    def owner_of(c):
        return lax.rem(c, owners), c // owners

    def part_copy(c, source, to_slot):
        q, k = owner_of(c)
        return remote(
            parts.at[c],
            gathered.at[to_slot, k, source],
            part_send_sem.at[c],
            part_recv_sem.at[to_slot, k, source],
            (half * members + q, host_row),
        )

    def own_tile(c):
        return both(is_host, m == owner_of(c)[0])

    edges = [zero] * row_tiles
    for c in order:
        pl.when(down_d)(depth_copy(c).wait_recv)
        cw = col_weights(c)
        absorb_c = absorb_of(c)
        for t in range(row_tiles):
            now, edges[t] = cols_mixed(rows_mixed(c, slab, t * SUB, row_weights(t)), edges[t], cw)
            depth = state[t, c, 1]
            carry = (jnp.exp2(depth), depth, state[t, c, 2])
            _, depth, light = shade(state[t, c, 0], now, carry, absorb_c)
            parts[c, 0, t * SUB : (t + 1) * SUB, :] = depth
            parts[c, 1, t * SUB : (t + 1) * SUB, :] = light

        @pl.when(jnp.logical_not(own_tile(c)))
        def _():
            part_copy(c, m, slot).start()

        @pl.when(own_tile(c))
        def _():
            gathered[hosts - 1, c // owners, pl.ds(m, 1)] = parts[pl.ds(c, 1)]

    def pair_copy(s, k, target, from_half, c):
        return remote(
            pairs.at[s, k],
            pair_in.at[from_half, c],
            pair_send_sem.at[s, k, target],
            pair_recv_sem.at[from_half, c],
            (target, host_row - hosts + 1 + s),
        )

    def factor_copy(s, k, j, c):
        return remote(
            factors.at[s, k, j],
            factor_in.at[c],
            factor_send_sem.at[s, k, j],
            factor_recv_sem.at[c],
            (half * members + j, host_row - hosts + 1 + s),
        )

    def elsewhere(s, j, body):
        if s == hosts - 1:
            pl.when(j != d)(body)
        else:
            body()

    def compose(k, s):
        mine = k * owners + m

        def arrived(j):
            elsewhere(
                s,
                half * members + j,
                lambda: remote(
                    parts.at[mine],
                    gathered.at[s, k, j],
                    part_send_sem.at[mine],
                    part_recv_sem.at[s, k, j],
                    (half * members + j, host_row),
                ).wait_recv(),
            )

        repeat(members, arrived)

        def add(j, carry):
            total, radiance = carry
            factor = jnp.exp2(total)
            factors[s, k, j] = factor
            return total + gathered[s, k, j, 0], radiance + factor * gathered[s, k, j, 1]

        blank = jnp.zeros((rows, LANES), jnp.float32)
        carry = (blank, blank)
        if members <= 16:
            for j in range(members):
                carry = add(j, carry)
        else:
            carry = lax.fori_loop(0, members, add, carry)
        pairs[s, k, 0] = carry[0]
        pairs[s, k, 1] = carry[1]

        def reply(target):
            elsewhere(s, target, lambda: pair_copy(s, k, target, half, mine).start())

        def reply_own(j):
            elsewhere(s, half * members + j, lambda: factor_copy(s, k, j, mine).start())

        repeat(n_depth, reply)
        repeat(members, reply_own)
        if s == hosts - 1:
            pair_in[half, mine] = pairs[s, k]
            factor_in[mine] = factors[s, k, m]

    @pl.when(is_owner)
    def _():
        for k in range(per_owner - 1, -1, -1):
            for s in range(hosts):
                compose(k, s)

    def from_other(c, h, body):
        q, _ = owner_of(c)
        pl.when(jnp.logical_not(both(is_host, d == h * members + q)))(body)

    for c in order:
        for h in range(HALVES):
            from_other(c, h, pair_copy(0, 0, d, h, c).wait_recv)
        pl.when(jnp.logical_not(own_tile(c)))(factor_copy(0, 0, m, c).wait_recv)
        where = slice(c * LANES, (c + 1) * LANES)
        before = jnp.exp2(pair_in[0, c, 0])
        ahead = jnp.where(half > 0, before, 1.0)
        front_ref[0, :, where] = ahead * factor_in[c]
        image_ref[0, :, where] = pair_in[0, c, 1] + before * pair_in[1, c, 1]
        image_ref[1, :, where] = before * jnp.exp2(pair_in[1, c, 0])

    @pl.when(up_d)
    def _():
        for c in order:
            depth_copy(c).wait_send()

    @pl.when(up_r)
    def _():
        for c in order:
            rows_copy(c).wait_send()

    pl.when(both(up_d, up_r))(corner_copy.wait_send)
    for c in order:
        pl.when(jnp.logical_not(own_tile(c)))(part_copy(c, m, slot).wait_send)

    @pl.when(is_owner)
    def _():
        for k in range(per_owner):
            for s in range(hosts):
                repeat(n_depth, lambda j: elsewhere(s, j, pair_copy(s, k, j, half, k * owners + m).wait_send))
                repeat(
                    members,
                    lambda j: elsewhere(s, half * members + j, factor_copy(s, k, j, k * owners + m).wait_send),
                )


def on_device(n_depth, n_rows, density, bin_of_level, absorb_bins, emit_bins, occupancy, col_offsets, row_offsets):
    slab, rows, cols = density.shape
    tiles = cols // LANES
    row_tiles = rows // SUB
    members = n_depth // HALVES
    hosts = 2 if n_rows % 2 == 0 else 1
    owners = 1
    while owners * 2 <= members and tiles % (owners * 2) == 0:
        owners *= 2
    per_owner = tiles // owners
    anywhere = pl.BlockSpec(memory_space=pl.ANY)
    vmem = pl.BlockSpec(memory_space=pltpu.VMEM)
    f32, i32 = jnp.float32, jnp.int32
    dma = pltpu.SemaphoreType.DMA
    return pl.pallas_call(
        functools.partial(kernel, n_depth, n_rows, hosts, owners),
        out_shape=(pltpu.VMEM((1, rows, cols), f32), pltpu.VMEM((2, rows, cols), f32)),
        in_specs=[anywhere] * 7,
        out_specs=(vmem, vmem),
        scratch_shapes=[
            pltpu.VMEM((tiles, slab + 1, rows + SUB, LANES), f32),
            pltpu.SMEM(bin_of_level.shape, i32),
            pltpu.SMEM(absorb_bins.shape, f32),
            pltpu.SMEM(emit_bins.shape, f32),
            pltpu.SMEM(occupancy.shape, i32),
            pltpu.VMEM((tiles, LANES), i32),
            pltpu.SMEM(row_offsets.shape, i32),
            pltpu.VMEM((tiles, slab, LANES), f32),
            pltpu.VMEM((tiles, slab, LANES), f32),
            pltpu.VMEM((tiles, LANES), f32),
            pltpu.VMEM((tiles, LANES), f32),
            pltpu.VMEM((slab, SUB, LANES), f32),
            pltpu.VMEM((row_tiles, tiles, 3, SUB, LANES), f32),
            pltpu.VMEM((tiles, 2, rows, LANES), f32),
            pltpu.VMEM((hosts, per_owner, members, 2, rows, LANES), f32),
            pltpu.VMEM((hosts, per_owner, members, rows, LANES), f32),
            pltpu.VMEM((hosts, per_owner, 2, rows, LANES), f32),
            pltpu.VMEM((tiles, rows, LANES), f32),
            pltpu.VMEM((HALVES, tiles, 2, rows, LANES), f32),
            dma((tiles,)),
            dma((6,)),
            dma((tiles,)),
            dma((tiles,)),
            dma((tiles,)),
            dma((tiles,)),
            dma((2,)),
            dma((tiles,)),
            dma((hosts, per_owner, members)),
            dma((hosts, per_owner, members)),
            dma((tiles,)),
            dma((hosts, per_owner, n_depth)),
            dma((HALVES, tiles)),
        ],
        compiler_params=pltpu.CompilerParams(collective_id=0, has_side_effects=True),
    )(
        density,
        bin_of_level,
        absorb_bins,
        emit_bins,
        occupancy,
        col_offsets.reshape(tiles, LANES),
        row_offsets,
    )


def solution(mesh):
    placed = (P("depth", "rows", None), P(), P(), P(), P("depth", "rows", None), P(), P("rows"))
    return jax.shard_map(
        functools.partial(on_device, mesh.shape["depth"], mesh.shape["rows"]),
        mesh=mesh,
        in_specs=placed,
        out_specs=(P("depth", "rows", None), P(None, "rows", None)),
        check_vma=False,
    )
```

time: 23.7 us -> 22.6 us (0.954)
  the two profiles are of different devices: /device:TPU:0 before, /device:TPU:1 now
where the time goes in v1:
time: 22.6 us; the launch traced here: 22.4 us
  Pallas kernels  20.5 us (91%)
  local copies, waits for them, and re-layouts  1.29 us (6%)
  between operations  0.64 us (3%)
    pallas_call x1, Pallas kernels, on_device(): pl.pallas_call(functools.partial(kernel, n_depth, n_rows, hosts, owners),...  20.5 us
    unnamed x2, local copies, waits for them, and re-layouts  1.29 us

profile of v1, /device:TPU:1, one launch (start us, length us, event | category | flops | bytes accessed | tf_op | source)
XLA Modules:
  0.0 22.4 jit_solution(10689681401016107274)
XLA Ops:
  0.6 20.5 %shard_map.86 = (f32[1,16,1024]{2,1,0:T(8,128)S(1)}, f32[2,16,1024]{2,1,0:T(8,128)S(1)}) custom-call(f32[16,16,1024]{2,1,0:T(8,128)} %dens_hbm.1, s32[16]{0:T(128)} %bins_hbm.1, f32[8]{0:T(128)} %absorb_hbm.1, f32[8]{0:T(128)} %emit_hbm.1, s32[1,1,8]{2,1,0:T(1,128)} %occ_hbm.1, s32[8,128]{1,0:T(8,128)} %bitcast.1, s32[16]{0:T(128)} %row_hbm.1), custom_call_target="tpu_custom_call" | custom-call | tf_op jit(solution)/shard_map/pallas_call | solution.py:511
  21.1 0.6 %copy.11 = f32[1,16,1024]{2,1,0:T(8,128)} copy(f32[1,16,1024]{2,1,0:T(8,128)S(1)} %get-tuple-element.2) | data formatting | bytes 131072
  21.8 0.7 %copy.12 = f32[2,16,1024]{2,1,0:T(8,128)} copy(f32[2,16,1024]{2,1,0:T(8,128)S(1)} %get-tuple-element.3) | data formatting | bytes 262144

commit v2 on v1

--- a/solution.py
+++ b/solution.py
@@ -72,8 +72,11 @@
     pairs,
     factor_in,
     pair_in,
+    first_sem,
+    rows_sem,
     load_sem,
     small_sem,
+    ready,
     depth_send_sem,
     depth_recv_sem,
     rows_send_sem,
@@ -101,10 +104,24 @@
     is_host = slot == hosts - 1
     is_owner = both(is_host, m < owners)
 
+    def first_load(c):
+        return pltpu.make_async_copy(
+            dens_hbm.at[0, :, pl.ds(c * LANES, LANES)],
+            dens.at[c, 0, pl.ds(0, rows), :],
+            first_sem.at[c],
+        )
+
+    def rows_load(c):
+        return pltpu.make_async_copy(
+            dens_hbm.at[:, 0, pl.ds(c * LANES, LANES)],
+            row_send.at[c],
+            rows_sem.at[c],
+        )
+
     def load(c):
         return pltpu.make_async_copy(
-            dens_hbm.at[:, :, c * LANES : (c + 1) * LANES],
-            dens.at[c, pl.ds(0, slab), pl.ds(0, rows), :],
+            dens_hbm.at[pl.ds(1, slab - 1), :, pl.ds(c * LANES, LANES)],
+            dens.at[c, pl.ds(1, slab - 1), pl.ds(0, rows), :],
             load_sem.at[c],
         )
 
@@ -121,44 +138,84 @@
             )
         )
     ]
+    barrier = pltpu.get_barrier_semaphore()
+    up_d, down_d = d > 0, d < n_depth - 1
+    up_r, down_r = r > 0, r < n_rows - 1
+
+    def greet(semaphore, dd, rr):
+        pl.semaphore_signal(semaphore, inc=1, device_id=(dd, rr), device_id_type=MESH)
+
+    for there, dd, rr in ((down_d, d + 1, r), (down_r, d, r + 1), (both(down_d, down_r), d + 1, r + 1)):
+        pl.when(there)(functools.partial(greet, barrier, dd, rr))
+
     order = list(range(tiles - 1, -1, -1))
+    for c in order:
+        first_load(c).start()
+    for c in order:
+        rows_load(c).start()
     for c in order:
         load(c).start()
     for copy in small:
         copy.start()
 
-    barrier = pltpu.get_barrier_semaphore()
-
-    def greet(dd, rr):
-        pl.semaphore_signal(barrier, inc=1, device_id=(dd, rr), device_id_type=MESH)
-
-    up_d, down_d = d > 0, d < n_depth - 1
-    up_r, down_r = r > 0, r < n_rows - 1
-    beside = (
-        (up_d, d - 1, r),
-        (up_r, d, r - 1),
-        (both(up_d, up_r), d - 1, r - 1),
-        (down_d, d + 1, r),
-        (down_r, d, r + 1),
-        (both(down_d, down_r), d + 1, r + 1),
-    )
-    expected = jnp.where(is_owner, n_depth * hosts - 1, HALVES * owners)
-    for there, dd, rr in beside:
-        pl.when(there)(functools.partial(greet, dd, rr))
+    def greet_block(semaphore, later):
+        for s in range(hosts):
+
+            def one(j, s=s):
+                wanted = is_owner
+                if s == hosts - 1:
+                    wanted = jnp.logical_or(wanted, lax.rem(j, members) < owners)
+                if later:
+                    side = jnp.logical_or(j > d, both(j == d, s > slot))
+                else:
+                    side = jnp.logical_or(j < d, both(j == d, s < slot))
+                pl.when(both(wanted, side))(
+                    functools.partial(greet, semaphore, jnp.int32(j), host_row - hosts + 1 + s)
+                )
+
+            repeat(n_depth, one)
+
+    greet_block(barrier, True)
+    earlier = jnp.where(is_owner, d * hosts + slot, half * owners + jnp.minimum(m, owners))
+    related = jnp.where(is_owner, n_depth * hosts - 1, HALVES * owners)
+    expected = earlier
+    for there in (up_d, up_r, both(up_d, up_r)):
         expected = expected + there.astype(jnp.int32)
 
-    for s in range(hosts):
-
-        def greet_block(j, s=s):
-            wanted = is_owner
-            if s == hosts - 1:
-                wanted = jnp.logical_or(wanted, lax.rem(j, members) < owners)
-            itself = both(j == d, slot == s)
-            pl.when(both(wanted, jnp.logical_not(itself)))(
-                functools.partial(greet, jnp.int32(j), host_row - hosts + 1 + s)
-            )
-
-        repeat(n_depth, greet_block)
+    def remote(src, dst, send_sem, recv_sem, device):
+        return pltpu.make_async_remote_copy(
+            src_ref=src,
+            dst_ref=dst,
+            send_sem=send_sem,
+            recv_sem=recv_sem,
+            device_id=device,
+            device_id_type=MESH,
+        )
+
+    def depth_copy(c):
+        return remote(
+            dens.at[c, 0, pl.ds(0, rows), :],
+            dens.at[c, slab, pl.ds(0, rows), :],
+            depth_send_sem.at[c],
+            depth_recv_sem.at[c],
+            (d - 1, r),
+        )
+
+    def rows_copy(c):
+        return remote(row_send.at[c], row_halo.at[c], rows_send_sem.at[c], rows_recv_sem.at[c], (d, r - 1))
+
+    corner_copy = remote(corner_send, corner, corner_sem.at[0], corner_sem.at[1], (d - 1, r - 1))
+
+    pl.when(expected > 0)(lambda: pl.semaphore_wait(barrier, expected))
+    for c in order:
+        first_load(c).wait()
+        pl.when(up_d)(depth_copy(c).start)
+    for c in order:
+        rows_load(c).wait()
+        corner_send[c : c + 1, :] = row_send[c, 0:1, :]
+        pl.when(up_r)(rows_copy(c).start)
+    greet_block(ready, False)
+    pl.when(both(up_d, up_r))(corner_copy.start)
 
     @pl.when(jnp.logical_not(down_d))
     def _():
@@ -253,7 +310,9 @@
         rw = row_weights(t)
         for z in range(slab):
             edge[z] = zero
-        for c in order:
+        for n, c in enumerate(order):
+            if t == row_tiles - 1 and n % 4 == 0:
+                fill_rows(order[n : n + 4])
             cw = col_weights(c)
             absorb_c = absorb_of(c)
             carry = (one, zero, zero)
@@ -270,64 +329,22 @@
 
     for c in order:
         load(c).wait()
-        for z in range(slab):
-            row_send[c, z : z + 1, :] = dens[c, z, 0:1, :]
-        corner_send[c : c + 1, :] = dens[c, 0, 0:1, :]
-
-    pl.semaphore_wait(barrier, expected)
-
-    def remote(src, dst, send_sem, recv_sem, device):
-        return pltpu.make_async_remote_copy(
-            src_ref=src,
-            dst_ref=dst,
-            send_sem=send_sem,
-            recv_sem=recv_sem,
-            device_id=device,
-            device_id_type=MESH,
-        )
-
-    def depth_copy(c):
-        return remote(
-            dens.at[c, 0, pl.ds(0, rows), :],
-            dens.at[c, slab, pl.ds(0, rows), :],
-            depth_send_sem.at[c],
-            depth_recv_sem.at[c],
-            (d - 1, r),
-        )
-
-    def rows_copy(c):
-        return remote(row_send.at[c], row_halo.at[c], rows_send_sem.at[c], rows_recv_sem.at[c], (d, r - 1))
-
-    corner_copy = remote(corner_send, corner, corner_sem.at[0], corner_sem.at[1], (d - 1, r - 1))
-
-    @pl.when(up_d)
-    def _():
-        for c in order:
-            depth_copy(c).start()
-
-    @pl.when(up_r)
-    def _():
-        for c in order:
-            rows_copy(c).start()
-
-    pl.when(both(up_d, up_r))(corner_copy.start)
+
+    def fill_rows(group_tiles):
+        @pl.when(down_r)
+        def _():
+            for c in group_tiles:
+                rows_copy(c).wait_recv()
+                for z in range(slab):
+                    dens[c, z, rows : rows + 1, :] = row_halo[c, z : z + 1, :]
+
+        @pl.when(jnp.logical_not(down_r))
+        def _():
+            for c in group_tiles:
+                for z in range(slab):
+                    dens[c, z, rows : rows + 1, :] = jnp.zeros((1, LANES), jnp.float32)
 
     for t in range(row_tiles):
-        if t == row_tiles - 1:
-
-            @pl.when(down_r)
-            def _():
-                for c in order:
-                    rows_copy(c).wait_recv()
-                    for z in range(slab):
-                        dens[c, z, rows : rows + 1, :] = row_halo[c, z : z + 1, :]
-
-            @pl.when(jnp.logical_not(down_r))
-            def _():
-                for c in order:
-                    for z in range(slab):
-                        dens[c, z, rows : rows + 1, :] = jnp.zeros((1, LANES), jnp.float32)
-
         march(t)
 
     @pl.when(both(down_d, down_r))
@@ -357,6 +374,7 @@
     def own_tile(c):
         return both(is_host, m == owner_of(c)[0])
 
+    pl.when(related > earlier)(lambda: pl.semaphore_wait(ready, related - earlier))
     edges = [zero] * row_tiles
     for c in order:
         pl.when(down_d)(depth_copy(c).wait_recv)
@@ -378,21 +396,21 @@
         def _():
             gathered[hosts - 1, c // owners, pl.ds(m, 1)] = parts[pl.ds(c, 1)]
 
-    def pair_copy(s, k, target, from_half, c):
+    def pair_copy(s, target, from_half, q):
         return remote(
-            pairs.at[s, k],
-            pair_in.at[from_half, c],
-            pair_send_sem.at[s, k, target],
-            pair_recv_sem.at[from_half, c],
+            pairs.at[s],
+            pair_in.at[from_half, q],
+            pair_send_sem.at[s, target],
+            pair_recv_sem.at[from_half, q],
             (target, host_row - hosts + 1 + s),
         )
 
-    def factor_copy(s, k, j, c):
+    def factor_copy(s, j, q):
         return remote(
-            factors.at[s, k, j],
-            factor_in.at[c],
-            factor_send_sem.at[s, k, j],
-            factor_recv_sem.at[c],
+            factors.at[s, j],
+            factor_in.at[q],
+            factor_send_sem.at[s, j],
+            factor_recv_sem.at[q],
             (half * members + j, host_row - hosts + 1 + s),
         )
 
@@ -423,7 +441,7 @@
         def add(j, carry):
             total, radiance = carry
             factor = jnp.exp2(total)
-            factors[s, k, j] = factor
+            factors[s, j, k] = factor
             return total + gathered[s, k, j, 0], radiance + factor * gathered[s, k, j, 1]
 
         blank = jnp.zeros((rows, LANES), jnp.float32)
@@ -436,38 +454,37 @@
         pairs[s, k, 0] = carry[0]
         pairs[s, k, 1] = carry[1]
 
-        def reply(target):
-            elsewhere(s, target, lambda: pair_copy(s, k, target, half, mine).start())
-
-        def reply_own(j):
-            elsewhere(s, half * members + j, lambda: factor_copy(s, k, j, mine).start())
-
+        if s == hosts - 1:
+            pair_in[half, m, k] = pairs[s, k]
+            factor_in[m, k] = factors[s, m, k]
+
+    rounds = [(k, s) for k in range(per_owner - 1, -1, -1) for s in range(hosts)]
+
+    def reply(target):
+        j = lax.rem(target, members)
+        for s in range(hosts):
+            pl.when(half == target // members)(lambda: elsewhere(s, target, factor_copy(s, j, m).start))
+            elsewhere(s, target, pair_copy(s, target, half, m).start)
+
+    @pl.when(is_owner)
+    def _():
+        for k, s in rounds:
+            compose(k, s)
         repeat(n_depth, reply)
-        repeat(members, reply_own)
-        if s == hosts - 1:
-            pair_in[half, mine] = pairs[s, k]
-            factor_in[mine] = factors[s, k, m]
-
-    @pl.when(is_owner)
-    def _():
-        for k in range(per_owner - 1, -1, -1):
-            for s in range(hosts):
-                compose(k, s)
-
-    def from_other(c, h, body):
-        q, _ = owner_of(c)
-        pl.when(jnp.logical_not(both(is_host, d == h * members + q)))(body)
-
-    for c in order:
+
+    for q in range(owners - 1, -1, -1):
         for h in range(HALVES):
-            from_other(c, h, pair_copy(0, 0, d, h, c).wait_recv)
-        pl.when(jnp.logical_not(own_tile(c)))(factor_copy(0, 0, m, c).wait_recv)
-        where = slice(c * LANES, (c + 1) * LANES)
-        before = jnp.exp2(pair_in[0, c, 0])
-        ahead = jnp.where(half > 0, before, 1.0)
-        front_ref[0, :, where] = ahead * factor_in[c]
-        image_ref[0, :, where] = pair_in[0, c, 1] + before * pair_in[1, c, 1]
-        image_ref[1, :, where] = before * jnp.exp2(pair_in[1, c, 0])
+            itself = both(is_host, d == h * members + q)
+            pl.when(jnp.logical_not(itself))(pair_copy(0, d, h, q).wait_recv)
+        pl.when(jnp.logical_not(both(is_host, m == q)))(factor_copy(0, m, q).wait_recv)
+        for k in range(per_owner):
+            c = k * owners + q
+            where = slice(c * LANES, (c + 1) * LANES)
+            before = jnp.exp2(pair_in[0, q, k, 0])
+            ahead = jnp.where(half > 0, before, 1.0)
+            front_ref[0, :, where] = ahead * factor_in[q, k]
+            image_ref[0, :, where] = pair_in[0, q, k, 1] + before * pair_in[1, q, k, 1]
+            image_ref[1, :, where] = before * jnp.exp2(pair_in[1, q, k, 0])
 
     @pl.when(up_d)
     def _():
@@ -485,13 +502,9 @@
 
     @pl.when(is_owner)
     def _():
-        for k in range(per_owner):
-            for s in range(hosts):
-                repeat(n_depth, lambda j: elsewhere(s, j, pair_copy(s, k, j, half, k * owners + m).wait_send))
-                repeat(
-                    members,
-                    lambda j: elsewhere(s, half * members + j, factor_copy(s, k, j, k * owners + m).wait_send),
-                )
+        for s in range(hosts):
+            repeat(n_depth, lambda j: elsewhere(s, j, pair_copy(s, j, half, m).wait_send))
+            repeat(members, lambda j: elsewhere(s, half * members + j, factor_copy(s, j, m).wait_send))
 
 
 def on_device(n_depth, n_rows, density, bin_of_level, absorb_bins, emit_bins, occupancy, col_offsets, row_offsets):
@@ -529,12 +542,15 @@
             pltpu.VMEM((row_tiles, tiles, 3, SUB, LANES), f32),
             pltpu.VMEM((tiles, 2, rows, LANES), f32),
             pltpu.VMEM((hosts, per_owner, members, 2, rows, LANES), f32),
-            pltpu.VMEM((hosts, per_owner, members, rows, LANES), f32),
+            pltpu.VMEM((hosts, members, per_owner, rows, LANES), f32),
             pltpu.VMEM((hosts, per_owner, 2, rows, LANES), f32),
-            pltpu.VMEM((tiles, rows, LANES), f32),
-            pltpu.VMEM((HALVES, tiles, 2, rows, LANES), f32),
+            pltpu.VMEM((owners, per_owner, rows, LANES), f32),
+            pltpu.VMEM((HALVES, owners, per_owner, 2, rows, LANES), f32),
+            dma((tiles,)),
+            dma((tiles,)),
             dma((tiles,)),
             dma((6,)),
+            pltpu.SemaphoreType.REGULAR,
             dma((tiles,)),
             dma((tiles,)),
             dma((tiles,)),
@@ -542,10 +558,10 @@
             dma((2,)),
             dma((tiles,)),
             dma((hosts, per_owner, members)),
-            dma((hosts, per_owner, members)),
-            dma((tiles,)),
-            dma((hosts, per_owner, n_depth)),
-            dma((HALVES, tiles)),
+            dma((hosts, members)),
+            dma((owners,)),
+            dma((hosts, n_depth)),
+            dma((HALVES, owners)),
         ],
         compiler_params=pltpu.CompilerParams(collective_id=0, has_side_effects=True),
     )(

time: 22.6 us -> 20.9 us (0.925)
  the two profiles are of different devices: /device:TPU:1 before, /device:TPU:11 now
where the time goes in v2:
time: 20.9 us; the launch traced here: 20.8 us
  Pallas kernels  18.9 us (90%)
  local copies, waits for them, and re-layouts  1.29 us (6%)
  between operations  0.64 us (3%)
    pallas_call x1, Pallas kernels, on_device(): pl.pallas_call(functools.partial(kernel, n_depth, n_rows, hosts, owners),...  18.9 us
    unnamed x2, local copies, waits for them, and re-layouts  1.29 us

profile of v2, /device:TPU:11, one launch (start us, length us, event | category | flops | bytes accessed | tf_op | source)
XLA Modules:
  0.0 20.8 jit_solution(15771606871225129325)
XLA Ops:
  0.6 18.9 %shard_map.86 = (f32[1,16,1024]{2,1,0:T(8,128)S(1)}, f32[2,16,1024]{2,1,0:T(8,128)S(1)}) custom-call(f32[16,16,1024]{2,1,0:T(8,128)} %dens_hbm.1, s32[16]{0:T(128)} %bins_hbm.1, f32[8]{0:T(128)} %absorb_hbm.1, f32[8]{0:T(128)} %emit_hbm.1, s32[1,1,8]{2,1,0:T(1,128)} %occ_hbm.1, s32[8,128]{1,0:T(8,128)} %bitcast.1, s32[16]{0:T(128)} %row_hbm.1), custom_call_target="tpu_custom_call" | custom-call | tf_op jit(solution)/shard_map/pallas_call | solution.py:524
  19.5 0.6 %copy.11 = f32[1,16,1024]{2,1,0:T(8,128)} copy(f32[1,16,1024]{2,1,0:T(8,128)S(1)} %get-tuple-element.2) | data formatting | bytes 131072
  20.1 0.7 %copy.12 = f32[2,16,1024]{2,1,0:T(8,128)} copy(f32[2,16,1024]{2,1,0:T(8,128)S(1)} %get-tuple-element.3) | data formatting | bytes 262144

commit v3 on v2

--- a/solution.py
+++ b/solution.py
@@ -108,21 +108,21 @@
         return pltpu.make_async_copy(
             dens_hbm.at[0, :, pl.ds(c * LANES, LANES)],
             dens.at[c, 0, pl.ds(0, rows), :],
-            first_sem.at[c],
+            first_sem,
         )
 
     def rows_load(c):
         return pltpu.make_async_copy(
             dens_hbm.at[:, 0, pl.ds(c * LANES, LANES)],
             row_send.at[c],
-            rows_sem.at[c],
+            rows_sem,
         )
 
     def load(c):
         return pltpu.make_async_copy(
             dens_hbm.at[pl.ds(1, slab - 1), :, pl.ds(c * LANES, LANES)],
             dens.at[c, pl.ds(1, slab - 1), pl.ds(0, rows), :],
-            load_sem.at[c],
+            load_sem,
         )
 
     small = [
@@ -138,6 +138,9 @@
             )
         )
     ]
+    def landed(ref, semaphore):
+        pltpu.make_async_copy(ref, ref, semaphore).wait()
+
     barrier = pltpu.get_barrier_semaphore()
     up_d, down_d = d > 0, d < n_depth - 1
     up_r, down_r = r > 0, r < n_rows - 1
@@ -148,6 +151,7 @@
     for there, dd, rr in ((down_d, d + 1, r), (down_r, d, r + 1), (both(down_d, down_r), d + 1, r + 1)):
         pl.when(there)(functools.partial(greet, barrier, dd, rr))
 
+    group = 4 if tiles % 4 == 0 else 1
     order = list(range(tiles - 1, -1, -1))
     for c in order:
         first_load(c).start()
@@ -196,24 +200,33 @@
         return remote(
             dens.at[c, 0, pl.ds(0, rows), :],
             dens.at[c, slab, pl.ds(0, rows), :],
-            depth_send_sem.at[c],
-            depth_recv_sem.at[c],
+            depth_send_sem,
+            depth_recv_sem.at[c // group],
             (d - 1, r),
         )
 
     def rows_copy(c):
-        return remote(row_send.at[c], row_halo.at[c], rows_send_sem.at[c], rows_recv_sem.at[c], (d, r - 1))
+        return remote(row_send.at[c], row_halo.at[c], rows_send_sem, rows_recv_sem.at[c // group], (d, r - 1))
 
     corner_copy = remote(corner_send, corner, corner_sem.at[0], corner_sem.at[1], (d - 1, r - 1))
 
     pl.when(expected > 0)(lambda: pl.semaphore_wait(barrier, expected))
+    landed(dens.at[:, 0, pl.ds(0, rows), :], first_sem)
+
+    @pl.when(up_d)
+    def _():
+        for c in order:
+            depth_copy(c).start()
+
+    landed(row_send, rows_sem)
     for c in order:
-        first_load(c).wait()
-        pl.when(up_d)(depth_copy(c).start)
-    for c in order:
-        rows_load(c).wait()
         corner_send[c : c + 1, :] = row_send[c, 0:1, :]
-        pl.when(up_r)(rows_copy(c).start)
+
+    @pl.when(up_r)
+    def _():
+        for c in order:
+            rows_copy(c).start()
+
     greet_block(ready, False)
     pl.when(both(up_d, up_r))(corner_copy.start)
 
@@ -311,8 +324,8 @@
         for z in range(slab):
             edge[z] = zero
         for n, c in enumerate(order):
-            if t == row_tiles - 1 and n % 4 == 0:
-                fill_rows(order[n : n + 4])
+            if t == row_tiles - 1 and n % group == 0:
+                fill_rows(order[n : n + group])
             cw = col_weights(c)
             absorb_c = absorb_of(c)
             carry = (one, zero, zero)
@@ -327,14 +340,15 @@
             state[t, c, 1] = carry[1]
             state[t, c, 2] = carry[2]
 
-    for c in order:
-        load(c).wait()
+    landed(dens.at[:, pl.ds(1, slab - 1), pl.ds(0, rows), :], load_sem)
 
     def fill_rows(group_tiles):
+        low = group_tiles[-1]
+
         @pl.when(down_r)
         def _():
+            landed(row_halo.at[pl.ds(low, group)], rows_recv_sem.at[low // group])
             for c in group_tiles:
-                rows_copy(c).wait_recv()
                 for z in range(slab):
                     dens[c, z, rows : rows + 1, :] = row_halo[c, z : z + 1, :]
 
@@ -366,8 +380,8 @@
         return remote(
             parts.at[c],
             gathered.at[to_slot, k, source],
-            part_send_sem.at[c],
-            part_recv_sem.at[to_slot, k, source],
+            part_send_sem,
+            part_recv_sem.at[to_slot, k],
             (half * members + q, host_row),
         )
 
@@ -377,7 +391,15 @@
     pl.when(related > earlier)(lambda: pl.semaphore_wait(ready, related - earlier))
     edges = [zero] * row_tiles
     for c in order:
-        pl.when(down_d)(depth_copy(c).wait_recv)
+        if (c + 1) % group == 0:
+
+            @pl.when(down_d)
+            def _(c=c):
+                landed(
+                    dens.at[pl.ds(c + 1 - group, group), slab, pl.ds(0, rows), :],
+                    depth_recv_sem.at[c // group],
+                )
+
         cw = col_weights(c)
         absorb_c = absorb_of(c)
         for t in range(row_tiles):
@@ -396,11 +418,12 @@
         def _():
             gathered[hosts - 1, c // owners, pl.ds(m, 1)] = parts[pl.ds(c, 1)]
 
-    def pair_copy(s, target, from_half, q):
+    def pair_copy(s, target, from_half, q, first=0, count=per_owner):
+        part = pl.ds(first, count)
         return remote(
-            pairs.at[s],
-            pair_in.at[from_half, q],
-            pair_send_sem.at[s, target],
+            pairs.at[s, part],
+            pair_in.at[from_half, q, part],
+            pair_send_sem.at[s, target // members],
             pair_recv_sem.at[from_half, q],
             (target, host_row - hosts + 1 + s),
         )
@@ -409,8 +432,8 @@
         return remote(
             factors.at[s, j],
             factor_in.at[q],
-            factor_send_sem.at[s, j],
-            factor_recv_sem.at[q],
+            factor_send_sem.at[s],
+            factor_recv_sem,
             (half * members + j, host_row - hosts + 1 + s),
         )
 
@@ -423,20 +446,10 @@
     def compose(k, s):
         mine = k * owners + m
 
-        def arrived(j):
-            elsewhere(
-                s,
-                half * members + j,
-                lambda: remote(
-                    parts.at[mine],
-                    gathered.at[s, k, j],
-                    part_send_sem.at[mine],
-                    part_recv_sem.at[s, k, j],
-                    (half * members + j, host_row),
-                ).wait_recv(),
-            )
-
-        repeat(members, arrived)
+        if s == hosts - 1:
+            landed(gathered.at[s, k, pl.ds(0, members - 1)], part_recv_sem.at[s, k])
+        else:
+            landed(gathered.at[s, k], part_recv_sem.at[s, k])
 
         def add(j, carry):
             total, radiance = carry
@@ -458,7 +471,7 @@
             pair_in[half, m, k] = pairs[s, k]
             factor_in[m, k] = factors[s, m, k]
 
-    rounds = [(k, s) for k in range(per_owner - 1, -1, -1) for s in range(hosts)]
+    ahead = 1
 
     def reply(target):
         j = lax.rem(target, members)
@@ -468,43 +481,64 @@
 
     @pl.when(is_owner)
     def _():
-        for k, s in rounds:
-            compose(k, s)
-        repeat(n_depth, reply)
-
+        for k in range(per_owner - 1, -1, -1):
+            for s in range(hosts):
+                compose(k, s)
+
+            def early(target, k=k):
+                for s in range(hosts):
+                    elsewhere(s, target, pair_copy(s, target, half, m, k, 1).start)
+
+            repeat(ahead, early)
+
+        def early_factor(target):
+            j = lax.rem(target, members)
+            for s in range(hosts):
+                pl.when(half == target // members)(lambda: elsewhere(s, target, factor_copy(s, j, m).start))
+
+        repeat(ahead, early_factor)
+        repeat(n_depth - ahead, lambda i: reply(i + ahead))
+
+    pl.when(is_owner)(lambda: landed(factor_in.at[pl.ds(0, owners - 1)], factor_recv_sem))
+    pl.when(jnp.logical_not(is_owner))(lambda: landed(factor_in, factor_recv_sem))
     for q in range(owners - 1, -1, -1):
         for h in range(HALVES):
             itself = both(is_host, d == h * members + q)
-            pl.when(jnp.logical_not(itself))(pair_copy(0, d, h, q).wait_recv)
-        pl.when(jnp.logical_not(both(is_host, m == q)))(factor_copy(0, m, q).wait_recv)
+            pl.when(jnp.logical_not(itself))(
+                functools.partial(landed, pair_in.at[h, q], pair_recv_sem.at[h, q])
+            )
         for k in range(per_owner):
             c = k * owners + q
             where = slice(c * LANES, (c + 1) * LANES)
             before = jnp.exp2(pair_in[0, q, k, 0])
-            ahead = jnp.where(half > 0, before, 1.0)
-            front_ref[0, :, where] = ahead * factor_in[q, k]
+            outside = jnp.where(half > 0, before, 1.0)
+            front_ref[0, :, where] = outside * factor_in[q, k]
             image_ref[0, :, where] = pair_in[0, q, k, 1] + before * pair_in[1, q, k, 1]
             image_ref[1, :, where] = before * jnp.exp2(pair_in[1, q, k, 0])
 
-    @pl.when(up_d)
-    def _():
-        for c in order:
-            depth_copy(c).wait_send()
-
-    @pl.when(up_r)
-    def _():
-        for c in order:
-            rows_copy(c).wait_send()
-
+    pl.when(up_d)(lambda: landed(dens.at[:, 0, pl.ds(0, rows), :], depth_send_sem))
+    pl.when(up_r)(lambda: landed(row_send, rows_send_sem))
     pl.when(both(up_d, up_r))(corner_copy.wait_send)
-    for c in order:
-        pl.when(jnp.logical_not(own_tile(c)))(part_copy(c, m, slot).wait_send)
+    pl.when(jnp.logical_not(is_owner))(lambda: landed(parts, part_send_sem))
 
     @pl.when(is_owner)
     def _():
+        landed(parts.at[pl.ds(0, tiles - per_owner)], part_send_sem)
         for s in range(hosts):
-            repeat(n_depth, lambda j: elsewhere(s, j, pair_copy(s, j, half, m).wait_send))
-            repeat(members, lambda j: elsewhere(s, half * members + j, factor_copy(s, j, m).wait_send))
+            others = members
+            if s == hosts - 1:
+                others = members - 1
+            landed(factors.at[s, pl.ds(0, others)], factor_send_sem.at[s])
+            for h in range(HALVES):
+                own = both(s == hosts - 1, half == h)
+                pl.when(own)(
+                    functools.partial(
+                        landed, gathered.at[s, :, pl.ds(0, members - 1)], pair_send_sem.at[s, h]
+                    )
+                )
+                pl.when(jnp.logical_not(own))(
+                    functools.partial(landed, gathered.at[s], pair_send_sem.at[s, h])
+                )
 
 
 def on_device(n_depth, n_rows, density, bin_of_level, absorb_bins, emit_bins, occupancy, col_offsets, row_offsets):
@@ -517,11 +551,12 @@
     while owners * 2 <= members and tiles % (owners * 2) == 0:
         owners *= 2
     per_owner = tiles // owners
+    groups = tiles // 4 if tiles % 4 == 0 else tiles
     anywhere = pl.BlockSpec(memory_space=pl.ANY)
     vmem = pl.BlockSpec(memory_space=pltpu.VMEM)
     f32, i32 = jnp.float32, jnp.int32
     dma = pltpu.SemaphoreType.DMA
-    return pl.pallas_call(
+    held = pl.pallas_call(
         functools.partial(kernel, n_depth, n_rows, hosts, owners),
         out_shape=(pltpu.VMEM((1, rows, cols), f32), pltpu.VMEM((2, rows, cols), f32)),
         in_specs=[anywhere] * 7,
@@ -546,21 +581,21 @@
             pltpu.VMEM((hosts, per_owner, 2, rows, LANES), f32),
             pltpu.VMEM((owners, per_owner, rows, LANES), f32),
             pltpu.VMEM((HALVES, owners, per_owner, 2, rows, LANES), f32),
-            dma((tiles,)),
-            dma((tiles,)),
-            dma((tiles,)),
+            dma,
+            dma,
+            dma,
             dma((6,)),
             pltpu.SemaphoreType.REGULAR,
-            dma((tiles,)),
-            dma((tiles,)),
-            dma((tiles,)),
-            dma((tiles,)),
+            dma,
+            dma((groups,)),
+            dma,
+            dma((groups,)),
             dma((2,)),
-            dma((tiles,)),
-            dma((hosts, per_owner, members)),
-            dma((hosts, members)),
-            dma((owners,)),
-            dma((hosts, n_depth)),
+            dma,
+            dma((hosts, per_owner)),
+            dma((hosts,)),
+            dma,
+            dma((hosts, HALVES)),
             dma((HALVES, owners)),
         ],
         compiler_params=pltpu.CompilerParams(collective_id=0, has_side_effects=True),
@@ -573,6 +608,24 @@
         col_offsets.reshape(tiles, LANES),
         row_offsets,
     )
+    return pl.pallas_call(
+        put_out,
+        out_shape=(jax.ShapeDtypeStruct((1, rows, cols), f32), jax.ShapeDtypeStruct((2, rows, cols), f32)),
+        in_specs=[vmem] * 2,
+        out_specs=(anywhere, anywhere),
+        scratch_shapes=[dma((2,))],
+    )(*(pltpu.with_memory_space_constraint(x, pltpu.VMEM) for x in held))
+
+
+def put_out(front, image, front_out, image_out, sem):
+    copies = [
+        pltpu.make_async_copy(front, front_out, sem.at[0]),
+        pltpu.make_async_copy(image, image_out, sem.at[1]),
+    ]
+    for copy in copies:
+        copy.start()
+    for copy in copies:
+        copy.wait()
 
 
 def solution(mesh):

time: 20.9 us -> 19.3 us (0.923)
  local copies, waits for them, and re-layouts: 1.29 us -> 0 us
  Pallas kernels: 18.9 us -> 18.5 us
    unnamed x2 -> x0, local copies, waits for them, and re-layouts: 1.29 us -> none
    pallas_call x1, Pallas kernels: 18.9 us -> 17.8 us  [on_device(): pl.pallas_call(functools.partial(kernel, n_depth, n_rows, hosts, owners),...]
    pallas_call x0 -> x1, Pallas kernels: none -> 0.7 us  [on_device(): pl.pallas_call(put_out, out_shape=(jax.ShapeDtypeStruct((1, rows, cols),...]
where the time goes in v3:
time: 19.3 us; the launch traced here: 19.2 us
  Pallas kernels  18.5 us (96%)
  between operations  0.64 us (3%)
    pallas_call x1, Pallas kernels, on_device(): pl.pallas_call(functools.partial(kernel, n_depth, n_rows, hosts, owners),...  17.8 us
    pallas_call x1, Pallas kernels, on_device(): pl.pallas_call(put_out, out_shape=(jax.ShapeDtypeStruct((1, rows, cols),...  0.7 us

profile of v3, /device:TPU:11, one launch (start us, length us, event | category | flops | bytes accessed | tf_op | source)
XLA Modules:
  0.0 19.2 jit_solution(10806165078797733496)
XLA Ops:
  0.6 17.8 %shard_map.86 = (f32[1,16,1024]{2,1,0:T(8,128)S(1)}, f32[2,16,1024]{2,1,0:T(8,128)S(1)}) custom-call(f32[16,16,1024]{2,1,0:T(8,128)} %dens_hbm.1, s32[16]{0:T(128)} %bins_hbm.1, f32[8]{0:T(128)} %absorb_hbm.1, f32[8]{0:T(128)} %emit_hbm.1, s32[1,1,8]{2,1,0:T(1,128)} %occ_hbm.1, s32[8,128]{1,0:T(8,128)} %bitcast.1, s32[16]{0:T(128)} %row_hbm.1), custom_call_target="tpu_custom_call" | custom-call | tf_op jit(solution)/shard_map/pallas_call | solution.py:559
  18.5 0.7 %shard_map.87 = (f32[1,16,1024]{2,1,0:T(8,128)}, f32[2,16,1024]{2,1,0:T(8,128)}) custom-call(f32[1,16,1024]{2,1,0:T(8,128)S(1)} %get-tuple-element.4.front, f32[2,16,1024]{2,1,0:T(8,128)S(1)} %get-tuple-element.5.image), custom_call_target="tpu_custom_call" | custom-call | tf_op jit(solution)/shard_map/pallas_call | solution.py:611

commit v4 on v3

--- a/solution.py
+++ b/solution.py
@@ -70,6 +70,8 @@
     gathered,
     factors,
     pairs,
+    finals,
+    crossed,
     factor_in,
     pair_in,
     first_sem,
@@ -88,6 +90,8 @@
     factor_recv_sem,
     pair_send_sem,
     pair_recv_sem,
+    cross_sem,
+    lead_sem,
 ):
     slab, rows, cols = dens_hbm.shape
     tiles = cols // LANES
@@ -213,10 +217,13 @@
     pl.when(expected > 0)(lambda: pl.semaphore_wait(barrier, expected))
     landed(dens.at[:, 0, pl.ds(0, rows), :], first_sem)
 
-    @pl.when(up_d)
-    def _():
+    at_once = jnp.logical_or(slot < hosts - 1, hosts == 1)
+
+    def send_depth():
         for c in order:
             depth_copy(c).start()
+
+    pl.when(both(up_d, at_once))(send_depth)
 
     landed(row_send, rows_sem)
     for c in order:
@@ -360,6 +367,8 @@
 
     for t in range(row_tiles):
         march(t)
+        if t == 0:
+            pl.when(both(up_d, jnp.logical_not(at_once)))(send_depth)
 
     @pl.when(both(down_d, down_r))
     def _():
@@ -418,12 +427,12 @@
         def _():
             gathered[hosts - 1, c // owners, pl.ds(m, 1)] = parts[pl.ds(c, 1)]
 
-    def pair_copy(s, target, from_half, q, first=0, count=per_owner):
+    def pair_copy(s, target, from_half, q, first=0, count=per_owner, send_sem=None):
         part = pl.ds(first, count)
         return remote(
             pairs.at[s, part],
             pair_in.at[from_half, q, part],
-            pair_send_sem.at[s, target // members],
+            pair_send_sem.at[s, 0] if send_sem is None else send_sem,
             pair_recv_sem.at[from_half, q],
             (target, host_row - hosts + 1 + s),
         )
@@ -468,53 +477,123 @@
         pairs[s, k, 1] = carry[1]
 
         if s == hosts - 1:
-            pair_in[half, m, k] = pairs[s, k]
-            factor_in[m, k] = factors[s, m, k]
-
-    ahead = 1
-
-    def reply(target):
+
+            @pl.when(half == 0)
+            def _():
+                pair_in[0, m, k] = pairs[s, k]
+                factor_in[m, k] = factors[s, m, k]
+
+    def reply_factor(target):
         j = lax.rem(target, members)
         for s in range(hosts):
-            pl.when(half == target // members)(lambda: elsewhere(s, target, factor_copy(s, j, m).start))
-            elsewhere(s, target, pair_copy(s, target, half, m).start)
+            elsewhere(s, half * members + j, factor_copy(s, j, m).start)
+
+    def reply(target, first=0, count=per_owner):
+        for s in range(hosts):
+            elsewhere(s, target, pair_copy(s, target, half, m, first, count).start)
+
+    def lead(k):
+        for s in range(hosts):
+            elsewhere(s, 0, pair_copy(s, 0, half, m, k, 1, lead_sem.at[s]).start)
+
+    def led():
+        for s in range(hosts):
+            elsewhere(s, 0, functools.partial(landed, pairs.at[s], lead_sem.at[s]))
+
+    def cross_copy(s):
+        return remote(
+            pairs.at[s],
+            crossed.at[s],
+            pair_send_sem.at[s, 1],
+            cross_sem.at[s],
+            (members + m, host_row),
+        )
+
+    def final_copy(s, j):
+        return remote(
+            finals.at[s],
+            pair_in.at[1, m],
+            pair_send_sem.at[s, 1],
+            pair_recv_sem.at[1, m],
+            (members + j, host_row - hosts + 1 + s),
+        )
+
+    def front_half():
+        reply_factor(0)
+        for s in range(hosts):
+            cross_copy(s).start()
+
+        def one(i):
+            reply_factor(i + 1)
+            reply(i + 1)
+
+        repeat(members - 1, one)
+
+    def back_half():
+        led()
+        split = (members - 1, members - 2) if members > 2 and False else ()
+        repeat(members - len(split) - 1, lambda i: reply(i + 1))
+        for k in range(per_owner - 1, -1, -1):
+            for target in split:
+                reply(target, k, 1)
+        for s in range(hosts):
+            landed(crossed.at[s], cross_sem.at[s])
+            for k in range(per_owner):
+                before = jnp.exp2(crossed[s, k, 0])
+                finals[s, k, 0] = crossed[s, k, 1] + before * pairs[s, k, 1]
+                finals[s, k, 1] = before * jnp.exp2(pairs[s, k, 0])
+
+                def scale(j, s=s, k=k, before=before):
+                    factors[s, j, k] = before * factors[s, j, k]
+
+                repeat(members, scale)
+
+            if s == hosts - 1:
+                pair_in[1, m] = finals[s]
+                factor_in[m] = factors[s, m]
+
+            def give(j, s=s):
+                elsewhere(s, members + j, final_copy(s, j).start)
+                elsewhere(s, members + j, factor_copy(s, j, m).start)
+
+            repeat(members, give)
 
     @pl.when(is_owner)
     def _():
         for k in range(per_owner - 1, -1, -1):
             for s in range(hosts):
                 compose(k, s)
-
-            def early(target, k=k):
-                for s in range(hosts):
-                    elsewhere(s, target, pair_copy(s, target, half, m, k, 1).start)
-
-            repeat(ahead, early)
-
-        def early_factor(target):
-            j = lax.rem(target, members)
-            for s in range(hosts):
-                pl.when(half == target // members)(lambda: elsewhere(s, target, factor_copy(s, j, m).start))
-
-        repeat(ahead, early_factor)
-        repeat(n_depth - ahead, lambda i: reply(i + ahead))
+            lead(k)
+        pl.when(half == 0)(front_half)
+        pl.when(half == 1)(back_half)
 
     pl.when(is_owner)(lambda: landed(factor_in.at[pl.ds(0, owners - 1)], factor_recv_sem))
     pl.when(jnp.logical_not(is_owner))(lambda: landed(factor_in, factor_recv_sem))
-    for q in range(owners - 1, -1, -1):
+    for q in range(owners):
         for h in range(HALVES):
-            itself = both(is_host, d == h * members + q)
-            pl.when(jnp.logical_not(itself))(
-                functools.partial(landed, pair_in.at[h, q], pair_recv_sem.at[h, q])
-            )
-        for k in range(per_owner):
-            c = k * owners + q
-            where = slice(c * LANES, (c + 1) * LANES)
-            before = jnp.exp2(pair_in[0, q, k, 0])
-            outside = jnp.where(half > 0, before, 1.0)
-            front_ref[0, :, where] = outside * factor_in[q, k]
-            image_ref[0, :, where] = pair_in[0, q, k, 1] + before * pair_in[1, q, k, 1]
-            image_ref[1, :, where] = before * jnp.exp2(pair_in[1, q, k, 0])
+            needed = jnp.logical_not(both(is_host, d == h * members + q))
+            if h == 0:
+                needed = both(needed, half == 0)
+            pl.when(needed)(functools.partial(landed, pair_in.at[h, q], pair_recv_sem.at[h, q]))
+
+        @pl.when(half == 0)
+        def _(q=q):
+            for k in range(per_owner):
+                c = k * owners + q
+                where = slice(c * LANES, (c + 1) * LANES)
+                before = jnp.exp2(pair_in[0, q, k, 0])
+                front_ref[0, :, where] = factor_in[q, k]
+                image_ref[0, :, where] = pair_in[0, q, k, 1] + before * pair_in[1, q, k, 1]
+                image_ref[1, :, where] = before * jnp.exp2(pair_in[1, q, k, 0])
+
+        @pl.when(half == 1)
+        def _(q=q):
+            for k in range(per_owner):
+                c = k * owners + q
+                where = slice(c * LANES, (c + 1) * LANES)
+                front_ref[0, :, where] = factor_in[q, k]
+                image_ref[0, :, where] = pair_in[1, q, k, 0]
+                image_ref[1, :, where] = pair_in[1, q, k, 1]
 
     pl.when(up_d)(lambda: landed(dens.at[:, 0, pl.ds(0, rows), :], depth_send_sem))
     pl.when(up_r)(lambda: landed(row_send, rows_send_sem))
@@ -529,16 +608,26 @@
             if s == hosts - 1:
                 others = members - 1
             landed(factors.at[s, pl.ds(0, others)], factor_send_sem.at[s])
-            for h in range(HALVES):
-                own = both(s == hosts - 1, half == h)
-                pl.when(own)(
-                    functools.partial(
-                        landed, gathered.at[s, :, pl.ds(0, members - 1)], pair_send_sem.at[s, h]
+
+            @pl.when(half == 0)
+            def _(s=s):
+                if s < hosts - 1:
+                    landed(gathered.at[s, :, pl.ds(0, members - 1)], pair_send_sem.at[s, 0])
+                else:
+                    pl.when(d == 0)(
+                        lambda: landed(gathered.at[s, :, pl.ds(0, members - 1)], pair_send_sem.at[s, 0])
                     )
-                )
-                pl.when(jnp.logical_not(own))(
-                    functools.partial(landed, gathered.at[s], pair_send_sem.at[s, h])
-                )
+                    pl.when(d > 0)(
+                        lambda: landed(gathered.at[s, :, pl.ds(0, members - 2)], pair_send_sem.at[s, 0])
+                    )
+                landed(pairs.at[s], pair_send_sem.at[s, 1])
+
+            @pl.when(half == 1)
+            def _(s=s, others=others):
+                landed(gathered.at[s, :, pl.ds(0, members - 1)], pair_send_sem.at[s, 0])
+                landed(gathered.at[s, :, pl.ds(0, others)], pair_send_sem.at[s, 1])
+
+        pl.when(half == 0)(led)
 
 
 def on_device(n_depth, n_rows, density, bin_of_level, absorb_bins, emit_bins, occupancy, col_offsets, row_offsets):
@@ -579,6 +668,8 @@
             pltpu.VMEM((hosts, per_owner, members, 2, rows, LANES), f32),
             pltpu.VMEM((hosts, members, per_owner, rows, LANES), f32),
             pltpu.VMEM((hosts, per_owner, 2, rows, LANES), f32),
+            pltpu.VMEM((hosts, per_owner, 2, rows, LANES), f32),
+            pltpu.VMEM((hosts, per_owner, 2, rows, LANES), f32),
             pltpu.VMEM((owners, per_owner, rows, LANES), f32),
             pltpu.VMEM((HALVES, owners, per_owner, 2, rows, LANES), f32),
             dma,
@@ -597,6 +688,8 @@
             dma,
             dma((hosts, HALVES)),
             dma((HALVES, owners)),
+            dma((hosts,)),
+            dma((hosts,)),
         ],
         compiler_params=pltpu.CompilerParams(collective_id=0, has_side_effects=True),
     )(

time: 19.3 us -> 19.3 us (level)
  no operation moved by 1% of the time
where the time goes in v4:
time: 19.3 us; the launch traced here: 19.1 us
  Pallas kernels  18.5 us (96%)
  between operations  0.64 us (3%)
    pallas_call x1, Pallas kernels, on_device(): pl.pallas_call(functools.partial(kernel, n_depth, n_rows, hosts, owners),...  17.8 us
    pallas_call x1, Pallas kernels, on_device(): pl.pallas_call(put_out, out_shape=(jax.ShapeDtypeStruct((1, rows, cols),...  0.7 us

profile of v4, /device:TPU:11, one launch (start us, length us, event | category | flops | bytes accessed | tf_op | source)
XLA Modules:
  0.0 19.1 jit_solution(8997419788657219594)
XLA Ops:
  0.6 17.8 %shard_map.86 = (f32[1,16,1024]{2,1,0:T(8,128)S(1)}, f32[2,16,1024]{2,1,0:T(8,128)S(1)}) custom-call(f32[16,16,1024]{2,1,0:T(8,128)} %dens_hbm.1, s32[16]{0:T(128)} %bins_hbm.1, f32[8]{0:T(128)} %absorb_hbm.1, f32[8]{0:T(128)} %emit_hbm.1, s32[1,1,8]{2,1,0:T(1,128)} %occ_hbm.1, s32[8,128]{1,0:T(8,128)} %bitcast.1, s32[16]{0:T(128)} %row_hbm.1), custom_call_target="tpu_custom_call" | custom-call | tf_op jit(solution)/shard_map/pallas_call | solution.py:648
  18.4 0.7 %shard_map.87 = (f32[1,16,1024]{2,1,0:T(8,128)}, f32[2,16,1024]{2,1,0:T(8,128)}) custom-call(f32[1,16,1024]{2,1,0:T(8,128)S(1)} %get-tuple-element.4.front, f32[2,16,1024]{2,1,0:T(8,128)S(1)} %get-tuple-element.5.image), custom_call_target="tpu_custom_call" | custom-call | tf_op jit(solution)/shard_map/pallas_call | solution.py:704

commit v5 on v4

--- a/solution.py
+++ b/solution.py
@@ -155,7 +155,7 @@
     for there, dd, rr in ((down_d, d + 1, r), (down_r, d, r + 1), (both(down_d, down_r), d + 1, r + 1)):
         pl.when(there)(functools.partial(greet, barrier, dd, rr))
 
-    group = 4 if tiles % 4 == 0 else 1
+    group = 2 if tiles % 2 == 0 else 1
     order = list(range(tiles - 1, -1, -1))
     for c in order:
         first_load(c).start()
@@ -640,7 +640,7 @@
     while owners * 2 <= members and tiles % (owners * 2) == 0:
         owners *= 2
     per_owner = tiles // owners
-    groups = tiles // 4 if tiles % 4 == 0 else tiles
+    groups = tiles // 2 if tiles % 2 == 0 else tiles
     anywhere = pl.BlockSpec(memory_space=pl.ANY)
     vmem = pl.BlockSpec(memory_space=pltpu.VMEM)
     f32, i32 = jnp.float32, jnp.int32

time: 19.3 us -> 19.3 us (level)
  no operation moved by 1% of the time
where the time goes in v5:
time: 19.3 us; the launch traced here: 19.2 us
  Pallas kernels  18.5 us (96%)
  between operations  0.64 us (3%)
    pallas_call x1, Pallas kernels, on_device(): pl.pallas_call(functools.partial(kernel, n_depth, n_rows, hosts, owners),...  17.8 us
    pallas_call x1, Pallas kernels, on_device(): pl.pallas_call(put_out, out_shape=(jax.ShapeDtypeStruct((1, rows, cols),...  0.7 us

profile of v5, /device:TPU:11, one launch (start us, length us, event | category | flops | bytes accessed | tf_op | source)
XLA Modules:
  0.0 19.2 jit_solution(16772241279100864837)
XLA Ops:
  0.6 17.8 %shard_map.86 = (f32[1,16,1024]{2,1,0:T(8,128)S(1)}, f32[2,16,1024]{2,1,0:T(8,128)S(1)}) custom-call(f32[16,16,1024]{2,1,0:T(8,128)} %dens_hbm.1, s32[16]{0:T(128)} %bins_hbm.1, f32[8]{0:T(128)} %absorb_hbm.1, f32[8]{0:T(128)} %emit_hbm.1, s32[1,1,8]{2,1,0:T(1,128)} %occ_hbm.1, s32[8,128]{1,0:T(8,128)} %bitcast.1, s32[16]{0:T(128)} %row_hbm.1), custom_call_target="tpu_custom_call" | custom-call | tf_op jit(solution)/shard_map/pallas_call | solution.py:648
  18.5 0.7 %shard_map.87 = (f32[1,16,1024]{2,1,0:T(8,128)}, f32[2,16,1024]{2,1,0:T(8,128)}) custom-call(f32[1,16,1024]{2,1,0:T(8,128)S(1)} %get-tuple-element.4.front, f32[2,16,1024]{2,1,0:T(8,128)S(1)} %get-tuple-element.5.image), custom_call_target="tpu_custom_call" | custom-call | tf_op jit(solution)/shard_map/pallas_call | solution.py:704
